TPU v7x, 32 devices: a whole 2x2x4 slice. The times are simulated.
32 devices in a mesh: shard: 4 (over z), ctx: 4 (over y, x), tp: 2 (over core).
Axes of the slice: x: 2, y: 2, z: 4, core: 2. Of those that a mesh axis runs over, the one named last changes fastest.
Arguments:
- hidden_in: bfloat16 [4, 512, 1536], P('shard', 'ctx'), may hold values from -6 to 6
- seg_start: int32 [4, 512], P('shard', 'ctx'), may hold values from 0 to 511, as said below
- norm1_gain: bfloat16 [1536], P('shard'), may hold values from 0.5 to 1.5
- w_qkv: bfloat16 [1536, 2, 8, 128], P('shard', 'tp'), may hold values from -0.15625 to 0.15625
- b_qkv: bfloat16 [128, 2, 8], P('shard', 'tp'), may hold values from -2 to 2
- w_attn_out: bfloat16 [1536, 1536], P('shard', 'tp'), may hold values from -0.875 to 0.875
- norm2_gain: bfloat16 [1536], P('shard'), may hold values from 0.5 to 1.5
- w_gate_up: bfloat16 [1536, 2, 8960], P('shard', None, 'tp'), may hold values from -0.15625 to 0.15625
- w_down: bfloat16 [1536, 8960], P('shard', 'tp'), may hold values from -0.0625 to 0.0625
- out_grad: bfloat16 [4, 512, 1536], P('shard', 'ctx'), may hold values from -6 to 6
Outputs:
- layer_out: float32 [4, 512, 1536], P('shard', 'ctx')
- in_grad: float32 [4, 512, 1536], P('shard', 'ctx')
- grad_norm1: float32 [1536], P('shard')
- grad_qkv: float32 [1536, 2, 8, 128], P('shard', 'tp')
- grad_bias: float32 [128, 2, 8], P('shard', 'tp')
- grad_attn_out: float32 [1536, 1536], P('shard', 'tp')
- grad_norm2: float32 [1536], P('shard')
- grad_gate_up: float32 [1536, 2, 8960], P('shard', None, 'tp')
- grad_down: float32 [1536, 8960], P('shard', 'tp')
Inputs may be any that keep to these rules, and one draw needn't show every extreme that they name: seg_start never falls along a row and equals its own position at a segment's first token; every segment holds 1 to 256 tokens, and every row has a segment of exactly 256 tokens.
All inputs are finite; a program needn't handle non-finite values.
Results may differ from a plain program's by a relative error of at most 0.02.
Values may be sent and summed in bfloat16 or wider, within the bound.
A program may use at most 320 MiB of HBM per device.

v0:
```python
import jax
import jax.numpy as jnp
from jax import lax
from jax.sharding import PartitionSpec as P

EPSILON = 1e-06
ROPE_BASE = 1000000.0
NEGATIVE = -1e30


def rope_tables(positions, head_dim):
    half_dim = head_dim // 2
    frequency = ROPE_BASE ** (-(jnp.arange(half_dim, dtype=jnp.float32) * 2.0) / head_dim)
    angles = positions[:, None] * frequency[None, :]
    cosine = jnp.cos(angles)
    sine_vals = jnp.sin(angles)
    return (jnp.concatenate([cosine, cosine], -1), jnp.concatenate([sine_vals, sine_vals], -1))


def rotate_half(values):
    half_dim = values.shape[-1] // 2
    return jnp.concatenate([-values[..., half_dim:], values[..., :half_dim]], -1)


def rotate_back(values):
    half_dim = values.shape[-1] // 2
    return jnp.concatenate([values[..., half_dim:], -values[..., :half_dim]], -1)


def apply_rope(values, cosine, sine_vals):
    return values * cosine + rotate_half(values) * sine_vals


def rope_grad(grads, cosine, sine_vals):
    return grads * cosine + rotate_back(grads * sine_vals)


def rms_back(grad_norm, inputs, inv_rms, gain_vals):
    scaled = gain_vals * grad_norm
    return inv_rms * scaled - inputs * (inv_rms * inv_rms * inv_rms) * jnp.mean(
        scaled * inputs, -1, keepdims=True
    )


def tensor_sum(partial_sum):
    return lax.psum(partial_sum, "tp")


def contract_rows(left, right):
    return lax.dot_general(
        left, right, (((0,), (0,)), ((), ())), preferred_element_type=jnp.float32
    )


def contract_cols(left, right):
    return lax.dot_general(
        left, right, (((1,), (1,)), ((), ())), preferred_element_type=jnp.float32
    )


def body(
    hidden_in,
    seg_start,
    norm1_gain,
    w_qkv,
    b_qkv,
    w_attn_out,
    norm2_gain,
    w_gate_up,
    w_down,
    out_grad,
):
    shards = lax.axis_size("shard")
    ctxs = lax.axis_size("ctx")
    ctx_id = lax.axis_index("ctx")
    tp_id = lax.axis_index("tp")
    everyone = ("shard", "ctx", "tp")
    bf16 = jnp.bfloat16
    qkv_full, attn_out_full, gain_one_bf, bias_full, gain_two_bf = (
        lax.all_gather(w_qkv, "shard", axis=0, tiled=True),
        lax.all_gather(w_attn_out, "shard", axis=0, tiled=True),
        lax.all_gather(norm1_gain, "shard", axis=0, tiled=True),
        lax.all_gather(b_qkv, "shard", axis=0, tiled=True),
        lax.all_gather(norm2_gain, "shard", axis=0, tiled=True),
    )
    tokens, width = (hidden_in.shape[1], hidden_in.shape[2])
    half = tokens // lax.axis_size("tp")
    part = w_gate_up.shape[0]
    hidden_units = w_down.shape[1] // (shards * ctxs)

    def my_units(weights):
        blocks = weights.reshape(weights.shape[:-1] + (ctxs, shards * hidden_units))
        return lax.dynamic_index_in_dim(blocks, ctx_id, weights.ndim - 1, keepdims=False)

    def my_half(rows):
        return lax.dynamic_slice_in_dim(rows, tp_id * half, half, 0)

    mine = jnp.concatenate([my_units(w_gate_up), my_units(w_down)[:, None]], 1)
    mine = jnp.transpose(mine.reshape(part, 3, shards, hidden_units), (2, 0, 1, 3))
    units = lax.all_to_all(mine, "shard", split_axis=0, concat_axis=0, tiled=True)
    units = units.reshape(shards * part, 3, hidden_units)
    gate_up_w = units[:, :2].reshape(shards * part, 2 * hidden_units)
    down_w = units[:, 2]
    grad_rows = out_grad[0]
    grad_all = lax.all_gather(my_half(grad_rows), everyone, axis=0, tiled=True)
    kv_local = qkv_full.shape[1]
    head_dim = qkv_full.shape[3]
    groups = qkv_full.shape[2] - 2
    query_scale = head_dim ** (-0.5)
    grad_scale = float(shards * ctxs * tokens) ** (-0.5)
    gain_one = gain_one_bf.astype(jnp.float32)
    gain_two = gain_two_bf.astype(jnp.float32)
    bias_vals = jnp.transpose(bias_full.astype(jnp.float32), (1, 2, 0))
    inputs = hidden_in[0].astype(jnp.float32)
    seg_row = seg_start[0]
    token_ids = ctx_id * tokens + jnp.arange(tokens, dtype=jnp.int32)
    cosine, sine_vals = rope_tables((token_ids - seg_row).astype(jnp.float32), head_dim)
    cos_four = cosine[:, None, None, :]
    sin_four = sine_vals[:, None, None, :]
    cos_three = cosine[:, None, :]
    sin_three = sine_vals[:, None, :]
    inv_rms1 = lax.rsqrt(jnp.mean(inputs * inputs, -1, keepdims=True) + EPSILON)
    normed1 = (inputs * inv_rms1 * gain_one).astype(bf16)
    qkv_vals = (
        jnp.einsum("td,dcsh->tcsh", normed1, qkv_full, preferred_element_type=jnp.float32)
        + bias_vals
    )
    q_rot = (apply_rope(qkv_vals[:, :, :groups], cos_four, sin_four) * query_scale).astype(bf16)
    k_rot = apply_rope(qkv_vals[:, :, groups], cos_three, sin_three).astype(bf16)
    v_vals = qkv_vals[:, :, groups + 1].astype(bf16)
    query_heads = jnp.transpose(q_rot, (1, 2, 0, 3))
    key_value = jnp.stack([k_rot, v_vals], axis=2)
    key_value = lax.all_gather(key_value, "ctx", axis=0, tiled=True)
    keys, values = (key_value[:, :, 0], key_value[:, :, 1])
    length = keys.shape[0]
    key_ids = jnp.arange(length, dtype=jnp.int32)
    allowed = (key_ids[None, :] <= token_ids[:, None]) & (key_ids[None, :] >= seg_row[:, None])
    scores = jnp.einsum("cgqh,kch->cgqk", query_heads, keys, preferred_element_type=jnp.float32)
    scores = jnp.where(allowed, scores, NEGATIVE)
    top_all = jnp.max(scores, -1, keepdims=True)
    raised = jnp.where(allowed, jnp.exp(scores - top_all), 0.0)
    total_all = jnp.sum(raised, -1, keepdims=True)
    attn_probs = raised / total_all
    probs_bf = attn_probs.astype(bf16)
    attn_vals = jnp.einsum(
        "cgqk,kch->cgqh", probs_bf, values, preferred_element_type=jnp.float32
    ).astype(bf16)
    attn_flat = jnp.transpose(attn_vals, (2, 0, 1, 3)).reshape(tokens, kv_local * groups * head_dim)
    resid1 = inputs + tensor_sum(contract_cols(attn_flat, attn_out_full))
    inv_rms2 = lax.rsqrt(jnp.mean(resid1 * resid1, -1, keepdims=True) + EPSILON)
    normed2 = (resid1 * inv_rms2 * gain_two).astype(bf16)
    normed2_all = lax.all_gather(my_half(normed2), everyone, axis=0, tiled=True)
    gate_up = jnp.dot(normed2_all, gate_up_w, preferred_element_type=jnp.float32)
    gate_vals, up_vals = (gate_up[:, :hidden_units], gate_up[:, hidden_units:])
    sigmoid_gate = jax.nn.sigmoid(gate_vals)
    silu_gate = gate_vals * sigmoid_gate
    hidden_act = (silu_gate * up_vals).astype(bf16)
    d_hidden = jnp.dot(grad_all, down_w, preferred_element_type=jnp.float32)
    d_gate = d_hidden * up_vals * sigmoid_gate * (1.0 + gate_vals * (1.0 - sigmoid_gate))
    d_up = d_hidden * silu_gate
    d_gate_up = jnp.concatenate([d_gate, d_up], 1).astype(bf16)

    def scatter_sum(partial_sum):
        share = lax.psum_scatter(
            partial_sum.astype(bf16), everyone, scatter_dimension=0, tiled=True
        )
        return lax.all_gather(share, "tp", axis=0, tiled=True).astype(jnp.float32)

    d_normed2 = scatter_sum(contract_cols(d_gate_up, gate_up_w))
    layer_out = resid1 + scatter_sum(contract_cols(hidden_act, down_w))
    grad_down = contract_rows(grad_all, hidden_act).astype(bf16)
    grad_gate_up = contract_rows(normed2_all, d_gate_up).astype(bf16)
    made = jnp.concatenate([grad_gate_up, grad_down], 1).reshape(shards, part, 3 * hidden_units)
    made = lax.all_to_all(made, "shard", split_axis=0, concat_axis=0, tiled=True)
    made = lax.all_gather(made, "ctx", axis=0, tiled=False)
    made = made.reshape(ctxs, shards, part, 3, hidden_units)
    made = jnp.transpose(made, (2, 3, 0, 1, 4)).reshape(part, 3, ctxs * shards * hidden_units)
    made = made.astype(jnp.float32) * grad_scale
    grad_norm2 = jnp.sum(d_normed2 * resid1 * inv_rms2, 0)
    d_resid1 = grad_rows.astype(jnp.float32) + rms_back(d_normed2, resid1, inv_rms2, gain_two)
    d_resid1_bf = d_resid1.astype(bf16)
    d_attn_flat = jnp.dot(d_resid1_bf, attn_out_full, preferred_element_type=jnp.float32)
    grad_attn_out = contract_rows(d_resid1_bf, attn_flat)
    d_attn = jnp.transpose(d_attn_flat.reshape(tokens, kv_local, groups, head_dim), (1, 2, 0, 3))
    delta_vals = jnp.sum(d_attn * attn_vals.astype(jnp.float32), -1)
    d_attn_bf = d_attn.astype(bf16)
    d_value = jnp.einsum("cgqk,cgqh->kch", probs_bf, d_attn_bf, preferred_element_type=jnp.float32)
    d_probs = jnp.einsum("cgqh,kch->cgqk", d_attn_bf, values, preferred_element_type=jnp.float32)
    d_scores = (attn_probs * (d_probs - delta_vals[..., None])).astype(bf16)
    d_query = jnp.einsum("cgqk,kch->cgqh", d_scores, keys, preferred_element_type=jnp.float32)
    d_key = jnp.einsum("cgqk,cgqh->kch", d_scores, query_heads, preferred_element_type=jnp.float32)
    key_grads = lax.psum_scatter(
        jnp.stack([d_key, d_value], 2).astype(bf16), "ctx", scatter_dimension=0, tiled=True
    ).astype(jnp.float32)
    d_query_rows = jnp.transpose(d_query, (2, 0, 1, 3))
    d_qkv = jnp.concatenate(
        [
            rope_grad(d_query_rows, cos_four, sin_four) * query_scale,
            rope_grad(key_grads[:, :, 0], cos_three, sin_three)[:, :, None],
            key_grads[:, :, 1][:, :, None],
        ],
        2,
    )
    grad_bias = jnp.transpose(jnp.sum(d_qkv, 0), (2, 0, 1))
    d_qkv_bf = d_qkv.astype(bf16)
    grad_qkv = jnp.einsum("td,tcsh->dcsh", normed1, d_qkv_bf, preferred_element_type=jnp.float32)
    d_normed1 = tensor_sum(
        jnp.einsum("tcsh,dcsh->td", d_qkv_bf, qkv_full, preferred_element_type=jnp.float32)
    )
    grad_norm1 = jnp.sum(d_normed1 * inputs * inv_rms1, 0)
    in_grad = d_resid1 + rms_back(d_normed1, inputs, inv_rms1, gain_one)

    def total(partial_sum):
        share = lax.psum_scatter(partial_sum.astype(bf16), "shard", scatter_dimension=0, tiled=True)
        return lax.psum(share, "ctx").astype(jnp.float32) * grad_scale

    return (
        layer_out[None],
        in_grad[None],
        total(grad_norm1),
        total(grad_qkv),
        total(grad_bias),
        total(grad_attn_out),
        total(grad_norm2),
        made[:, :2],
        made[:, 2],
    )


def solution(mesh):
    in_specs = (
        P("shard", "ctx", None),
        P("shard", "ctx"),
        P("shard"),
        P("shard", "tp", None, None),
        P("shard", "tp", None),
        P("shard", "tp"),
        P("shard"),
        P("shard", None, "tp"),
        P("shard", "tp"),
        P("shard", "ctx", None),
    )
    out_specs = (
        P("shard", "ctx", None),
        P("shard", "ctx", None),
        P("shard"),
        P("shard", "tp", None, None),
        P("shard", "tp", None),
        P("shard", "tp"),
        P("shard"),
        P("shard", None, "tp"),
        P("shard", "tp"),
    )
    return jax.shard_map(body, mesh=mesh, in_specs=in_specs, out_specs=out_specs, check_vma=False)
```

profile of v0, /device:TPU:0, one launch (start us, length us, event | category | flops | bytes accessed | tf_op | source)
XLA Modules:
  0.0 1046.7 jit_solution(12587943593719788081)
XLA Ops:
  7.3 2.5 copy.67
  10.6 13.6 %all-gather.2 = bf16[4,1,384]{2,1,0:T(2,128)(2,1)S(1)} all-gather(bf16[1,1,384]{2,1,0:T(2,128)(2,1)S(1)} %reshape.562), channel_id=1, replica_groups=mesh['shard'=4,'ctx'=4,'tp'=2] {'shard'}, dimensions={0}, use_global_device_ids=true | all-gather | bytes 3840 | tf_op jit(solution)/shard_map/all_gather | solution.py:82
  25.2 15.2 %all_gather.38 = bf16[128,1,8]{2,1,0:T(2,128)(2,1)S(1)} all-gather(bf16[32,1,8]{2,1,0:T(2,128)(2,1)S(1)} %copy.68), channel_id=1, replica_groups=mesh['shard'=4,'ctx'=4,'tp'=2] {'shard'}, dimensions={0}, use_global_device_ids=true | all-gather | bytes 2560 | tf_op jit(solution)/shard_map/all_gather | solution.py:83
  41.7 35.5 %all-gather.10.cloned.1.call-done = bf16[1536,1,8,128]{0,3,2,1:T(8,128)(2,1)} async-done(((bf16[384,1,8,128]{0,3,2,1:T(8,128)(2,1)}), bf16[1536,1,8,128]{0,3,2,1:T(8,128)(2,1)}) %all-gather.10.cloned.1.call-update) | async-done | bytes 3145744 | tf_op jit(solution)/shard_map/all_gather | solution.py:80
  77.1 2.9 fusion.47
  80.4 8.9 all_gather.39
  90.9 36.5 %all-gather.12.cloned.1.call-done = bf16[1536,768]{1,0:T(8,128)(2,1)} async-done(((bf16[384,768]{1,0:T(8,128)(2,1)}), bf16[1536,768]{1,0:T(8,128)(2,1)}) %all-gather.12.cloned.1.call-update) | async-done | bytes 2359312 | tf_op jit(solution)/shard_map/all_gather | solution.py:81
  127.3 3.4 fusion.90
  130.9 12.1 %all-gather.3 = bf16[4,1,384]{2,1,0:T(2,128)(2,1)S(1)} all-gather(bf16[1,1,384]{2,1,0:T(2,128)(2,1)S(1)} %reshape.564), channel_id=1, replica_groups=mesh['shard'=4,'ctx'=4,'tp'=2] {'shard'}, dimensions={0}, use_global_device_ids=true | all-gather | bytes 3840 | tf_op jit(solution)/shard_map/all_gather | solution.py:84
  143.0 5.7 all-reduce.9.cloned.1.call-done
  152.3 5.9 copy.73
  158.1 18.0 %copy.72 = bf16[384,2,4480]{0,2,1:T(8,128)(2,1)} copy(bf16[384,2,4480]{2,1,0:T(2,128)(2,1)} %param.17) | data formatting | bytes 13762560 | tf_op args[7]
  179.6 85.7 %all_to_all.10 = bf16[4,384,3,280]{1,3,2,0:T(8,128)(2,1)S(1)} all-to-all(bf16[4,384,3,280]{1,3,2,0:T(8,128)(2,1)S(1)} %copy.74), channel_id=1, replica_groups=mesh['shard'=4,'ctx'=4,'tp'=2] {'shard'}, dimensions={0} | all-to-all | bytes 5160960 | tf_op jit(solution)/shard_map/all_to_all | solution.py:100
  268.4 9.2 fusion.91
  277.5 42.8 %all-gather.16.cloned.1.call-done = bf16[1,2048,1536]{2,1,0:T(8,128)(2,1)} async-done(((bf16[1,64,1536]{2,1,0:T(8,128)(2,1)}), bf16[1,2048,1536]{2,1,0:T(8,128)(2,1)}) %all-gather.16.cloned.1.call-update) | async-done | bytes 6291472 | tf_op jit(solution)/shard_map/all_gather | solution.py:105
  320.4 8.1 multiply_convert_fusion.1
  329.8 7.0 convolution_convert_fusion
  336.9 7.7 convolution_convert_fusion.1
  344.7 105.9 %reduce-scatter.13.cloned.1.call-done = bf16[64,1536]{1,0:T(8,128)(2,1)} async-done(((bf16[2048,1536]{1,0:T(8,128)(2,1)}), bf16[64,1536]{1,0:T(8,128)(2,1)}) %reduce-scatter.13.cloned.1.call-update) | async-done | bytes 196624 | tf_op jit(solution)/shard_map/reduce_scatter | solution.py:164
  450.5 2.3 all_gather.45
  454.2 116.5 %reduce-scatter.11.cloned.1.call-done = bf16[64,1536]{1,0:T(8,128)(2,1)} async-done(((bf16[2048,1536]{1,0:T(8,128)(2,1)}), bf16[64,1536]{1,0:T(8,128)(2,1)}) %reduce-scatter.11.cloned.1.call-update) | async-done | bytes 196624 | tf_op jit(solution)/shard_map/reduce_scatter | solution.py:164
  570.7 2.5 all_gather.43
  573.2 2.3 fusion.29
  575.5 3.0 fusion.66
  580.5 2.2 convolution_convert_fusion.3
  584.5 19.4 %reduce-scatter.19.cloned.1.call-done = bf16[128,256]{1,0:T(8,128)(2,1)} async-done(((bf16[512,256]{1,0:T(8,128)(2,1)}), bf16[128,256]{1,0:T(8,128)(2,1)}) %reduce-scatter.19.cloned.1.call-update) | async-done | bytes 65552
  606.2 2.7 fusion.5
  610.2 5.3 fusion.8
  615.6 6.5 convolution_convert_fusion.4
  624.0 4.8 all-to-all-start.1
  631.7 2.5 fusion.11
  634.2 43.2 %reduce-scatter.17.cloned.1.call-done = bf16[384,768]{1,0:T(8,128)(2,1)} async-done(((bf16[1536,768]{1,0:T(8,128)(2,1)}), bf16[384,768]{1,0:T(8,128)(2,1)}) %reduce-scatter.17.cloned.1.call-update) | async-done | bytes 589840 | tf_op jit(solution)/shard_map/reduce_scatter | solution.py:214
  677.4 82.8 %reduce-scatter.15.cloned.1.call-done = bf16[384,1,8,128]{3,0,2,1:T(8,128)(2,1)} async-done(((bf16[1536,1,8,128]{3,0,2,1:T(8,128)(2,1)}), bf16[384,1,8,128]{3,0,2,1:T(8,128)(2,1)}) %reduce-scatter.15.cloned.1.call-update) | async-done | bytes 786448 | tf_op jit(solution)/shard_map/reduce_scatter | solution.py:214
  762.0 19.3 %reduce-scatter.21.cloned.1.call-done = bf16[32,8]{1,0:T(8,128)(2,1)} async-done(((bf16[128,8]{1,0:T(8,128)(2,1)}), bf16[32,8]{1,0:T(8,128)(2,1)}) %reduce-scatter.21.cloned.1.call-update) | async-done | bytes 528
  782.1 19.1 %all-reduce.11.cloned.1.call-done = f32[128,1536]{1,0:T(8,128)} async-done(((f32[128,1536]{1,0:T(8,128)}), f32[128,1536]{1,0:T(8,128)}) %all-reduce.11.cloned.1.call-update) | async-done | bytes 786448 | tf_op jit(solution)/shard_map/psum | solution.py:46
  802.6 12.2 %all-reduce.4 = (bf16[1536]{0:T(1024)(128)(2,1)S(1)}, bf16[1536]{0:T(1024)(128)(2,1)S(1)}) all-reduce(bf16[1536]{0:T(1024)(128)(2,1)S(1)} %get-tuple-element.47, bf16[1536]{0:T(1024)(128)(2,1)S(1)} %copy-done.24), channel_id=7, replica_groups=mesh['shard'=4,'ctx'=4,'tp'=2] {'shard'}, use_global_device_ids=true, to_apply=%region_13.14.clone | all-reduce | flops 3072 | bytes 12288
  814.9 10.1 all-reduce.2
  826.7 2.4 fusion.37
  829.1 34.2 %all-reduce.13.cloned.1.call-done = (bf16[384,1,8,128]{3,0,2,1:T(8,128)(2,1)}, bf16[384,768]{1,0:T(8,128)(2,1)}) async-done(((bf16[384,1,8,128]{3,0,2,1:T(8,128)(2,1)}, bf16[384,768]{1,0:T(8,128)(2,1)}), (bf16[384,1,8,128]{3,0,2,1:T(8,128)(2,1)}, bf16[384,768]{1,0:T(8,128)(2,1)})) %all-reduce.13.cloned.1.call-update) | async-done | bytes 1376272 | tf_op jit(solution)/shard_map/psum | solution.py:215
  864.6 2.1 copy.85
  867.8 100.8 %all-gather.18.cloned.1.call-done = bf16[16,384,840]{1,2,0:T(8,128)(2,1)} async-done(((bf16[4,384,840]{1,2,0:T(8,128)(2,1)}), bf16[16,384,840]{1,2,0:T(8,128)(2,1)}) %all-gather.18.cloned.1.call-update) | async-done | bytes 10321936 | tf_op jit(solution)/shard_map/all_gather | solution.py:175
  968.6 12.6 %convert_multiply_fusion = f32[16,384,840]{1,2,0:T(8,128)} fusion(bf16[16,384,840]{1,2,0:T(8,128)(2,1)} %all-gather.18.cloned.1.call-done), kind=kLoop, calls=%fused_computation.1 | loop fusion | flops 10321920 | bytes 30965760 | tf_op jit(solution)/shard_map/mul | solution.py:178
  981.2 8.2 copy.84
  989.5 6.9 copy-done
  996.3 3.2 slice_bitcast_fusion
  999.5 10.7 %slice.106 = f32[384,2,4480]{0,2,1:T(8,128)} slice(f32[384,3,4480]{0,2,1:T(8,128)} %bitcast.226), slice={[0:384], [0:2], [0:4480]} | slice | bytes 27525120 | tf_op jit(solution)/shard_map/slice | solution.py:225
  1010.2 21.5 %copy.86 = f32[384,2,4480]{2,1,0:T(2,128)} copy(f32[384,2,4480]{0,2,1:T(8,128)} %slice.106) | data formatting | bytes 27525120
  1031.7 8.4 copy.87
  (185 shorter events, 37.3 us)
Async XLA Ops:
  7.2 3.4 copy-start.31
  7.2 17.1 %copy-start.33 = (s32[1,128]{1,0:T(1,128)S(1)}, s32[1,128]{1,0:T(1,128)}, u32[]{:S(2)}) copy-start(s32[1,128]{1,0:T(1,128)} %param.11) | copy-start | bytes 1540
  7.2 18.0 %copy-start.30 = (bf16[32,1,8]{0,2,1:T(8,128)(2,1)S(1)}, bf16[32,1,8]{0,2,1:T(8,128)(2,1)}, u32[]{:S(2)}) copy-start(bf16[32,1,8]{0,2,1:T(8,128)(2,1)} %param.14) | copy-start | bytes 1540
  7.2 33.3 %copy-start.1 = (bf16[1,128,1536]{2,1,0:T(8,128)(2,1)S(1)}, bf16[1,128,1536]{2,1,0:T(8,128)(2,1)}, u32[]{:S(2)}) copy-start(bf16[1,128,1536]{2,1,0:T(8,128)(2,1)} %param.10) | copy-start | bytes 1179652
  7.2 69.9 %all-gather.10.cloned.1.call-start = ((), (), s32[]{:S(2)}) async-start(), calls=%async_computation.8 | async-start | bytes 3932160 | tf_op jit(solution)/shard_map/all_gather | solution.py:80
  9.8 117.6 %all-gather.12.cloned.1.call-start = ((), (), s32[]{:S(2)}) async-start(), calls=%async_computation.9 | async-start | bytes 2949120 | tf_op jit(solution)/shard_map/all_gather | solution.py:81
  10.5 138.2 %all-reduce.9.cloned.1.call-start = ((), (), s32[]{:S(2)}) async-start(), calls=%async_computation.10 | async-start | bytes 1572864 | tf_op jit(solution)/shard_map/psum | solution.py:46
  25.1 64.2 %copy-start.14 = (f32[128,128]{0,1:T(8,128)}, f32[128,128]{0,1:T(8,128)S(1)}, u32[]{:S(2)}) copy-start(f32[128,128]{0,1:T(8,128)S(1)} %get-tuple-element.85) | copy-start | bytes 196612
  25.1 64.2 %copy-start.17 = (f32[128,128]{0,1:T(8,128)}, f32[128,128]{0,1:T(8,128)S(1)}, u32[]{:S(2)}) copy-start(f32[128,128]{0,1:T(8,128)S(1)} %get-tuple-element.86) | copy-start | bytes 196612
  41.3 39.0 %copy-start.25 = (f32[128]{0:T(128)}, f32[128]{0:T(128)S(1)}, u32[]{:S(2)}) copy-start(f32[128]{0:T(128)S(1)} %get-tuple-element.80) | copy-start | bytes 1540
  41.5 38.8 %copy-start.21 = (f32[128,1,1,64]{0,3,2,1:T(8,128)}, f32[128,1,1,64]{0,3,2,1:T(8,128)S(1)}, u32[]{:S(2)}) copy-start(f32[128,1,1,64]{0,3,2,1:T(8,128)S(1)} %multiply_cosine_fusion.1) | copy-start | bytes 98308
  90.3 37.1 %copy-start.27 = (f32[6,128]{1,0:T(8,128)}, f32[6,128]{1,0:T(8,128)S(1)}, u32[]{:S(2)}) copy-start(f32[6,128]{1,0:T(8,128)S(1)} %get-tuple-element.83) | copy-start | bytes 9220
  90.3 40.5 %copy-start.8 = (f32[6,128,512]{2,1,0:T(8,128)}, f32[6,128,512]{2,1,0:T(8,128)S(1)}, u32[]{:S(2)}) copy-start(f32[6,128,512]{2,1,0:T(8,128)S(1)} %get-tuple-element.84) | copy-start | bytes 4718596
  90.5 40.4 %copy-start.32 = (bf16[384]{0:T(512)(128)(2,1)S(1)}, bf16[384]{0:T(512)(128)(2,1)}, u32[]{:S(2)}) copy-start(bf16[384]{0:T(512)(128)(2,1)} %param.16) | copy-start | bytes 2308
  130.8 20.7 %copy-start.12 = (bf16[1,128,1536]{2,1,0:T(8,128)(2,1)S(1)}, bf16[1,128,1536]{2,1,0:T(8,128)(2,1)}, u32[]{:S(2)}) copy-start(bf16[1,128,1536]{2,1,0:T(8,128)(2,1)} %param.19) | copy-start | bytes 1179652
  130.8 137.5 %all-gather.14.cloned.1.call-start = ((), (), s32[]{:S(2)}) async-start(), calls=%async_computation.11 | async-start | bytes 6488064 | tf_op jit(solution)/shard_map/all_gather | solution.py:152
  150.5 302.3 %copy-start.29 = (f32[128]{0:T(128)}, f32[128]{0:T(128)S(1)}, u32[]{:S(2)}) copy-start(f32[128]{0:T(128)S(1)} %get-tuple-element.82) | copy-start | bytes 1540
  151.4 168.9 %all-gather.16.cloned.1.call-start = ((), (), s32[]{:S(2)}) async-start(), calls=%async_computation.17 | async-start | bytes 6488064 | tf_op jit(solution)/shard_map/all_gather | solution.py:105
  152.2 298.3 %reduce-scatter.13.cloned.1.call-start = ((), (), s32[]{:S(2)}) async-start(), calls=%async_computation.13 | async-start | bytes 6488064 | tf_op jit(solution)/shard_map/reduce_scatter | solution.py:164
  265.6 1.5 copy-start.5
  320.4 9.4 copy-start.7
  336.8 233.9 %reduce-scatter.11.cloned.1.call-start = ((), (), s32[]{:S(2)}) async-start(), calls=%async_computation.12 | async-start | bytes 6488064 | tf_op jit(solution)/shard_map/reduce_scatter | solution.py:164
  344.6 259.3 %reduce-scatter.19.cloned.1.call-start = ((), (), s32[]{:S(2)}) async-start(), calls=%async_computation.19 | async-start | bytes 327680
  575.5 5.0 copy-start.3
  575.5 3.4 copy-start.9
  575.5 3.4 copy-start.11
  575.5 3.4 copy-start.28
  580.5 97.0 %reduce-scatter.17.cloned.1.call-start = ((), (), s32[]{:S(2)}) async-start(), calls=%async_computation.16 | async-start | bytes 2949120 | tf_op jit(solution)/shard_map/reduce_scatter | solution.py:214
  582.8 22.2 %copy-start.23 = (f32[128,1,64]{0,2,1:T(8,128)S(1)}, f32[128,1,64]{0,2,1:T(8,128)}, u32[]{:S(2)}) copy-start(f32[128,1,64]{0,2,1:T(8,128)} %get-tuple-element.75) | copy-start | bytes 98308
  582.8 22.2 %copy-start.22 = (f32[128,1,1,64]{0,3,2,1:T(8,128)S(1)}, f32[128,1,1,64]{0,3,2,1:T(8,128)}, u32[]{:S(2)}) copy-start(f32[128,1,1,64]{0,3,2,1:T(8,128)} %copy-done.21) | copy-start | bytes 98308
  582.8 23.4 %copy-start.26 = (f32[128]{0:T(128)S(1)}, f32[128]{0:T(128)}, u32[]{:S(2)}) copy-start(f32[128]{0:T(128)} %copy-done.25) | copy-start | bytes 1540
  582.8 177.4 %reduce-scatter.15.cloned.1.call-start = ((), (), s32[]{:S(2)}) async-start(), calls=%async_computation.15 | async-start | bytes 3932160 | tf_op jit(solution)/shard_map/reduce_scatter | solution.py:214
  584.5 24.5 %copy-start.6 = (bf16[128,6,128]{0,2,1:T(8,128)(2,1)}, bf16[128,6,128]{0,2,1:T(8,128)(2,1)S(1)}, u32[]{:S(2)}) copy-start(bf16[128,6,128]{0,2,1:T(8,128)(2,1)S(1)} %get-tuple-element.56) | copy-start | bytes 589828
  604.9 4.1 copy-start.16
  610.2 5.3 copy-start.38
  610.2 5.3 copy-start.40
  624.0 7.7 copy-start.2
  624.0 136.3 %all-to-all-start.1 = ((bf16[4,384,840]{1,2,0:T(8,128)(2,1)}), bf16[4,384,840]{1,2,0:T(8,128)(2,1)}, u32[]{:S(2)}, u32[]{:S(2)}) async-start(bf16[4,384,840]{1,2,0:T(8,128)(2,1)} %bitcast.230), calls=%async_computation.5 | async-start | bytes 5160960 | tf_op jit(solution)/shard_map/all_to_all | solution.py:174
  628.8 152.5 %reduce-scatter.21.cloned.1.call-start = ((), (), s32[]{:S(2)}) async-start(), calls=%async_computation.20 | async-start | bytes 40960
  631.6 169.6 %all-reduce.11.cloned.1.call-start = ((), (), s32[]{:S(2)}) async-start(), calls=%async_computation.14 | async-start | bytes 1572864 | tf_op jit(solution)/shard_map/psum | solution.py:46
  634.1 126.7 %copy-start.35 = (u32[32]{0:T(128)S(1)}, u32[32]{0:T(128)}, u32[]{:S(2)}) copy-start(u32[32]{0:T(128)} %constant.62) | copy-start | bytes 388
  634.2 229.1 %all-reduce.13.cloned.1.call-start = ((), (), s32[]{:S(2)}) async-start(), calls=%async_computation.21 | async-start | bytes 2752512 | tf_op jit(solution)/shard_map/psum | solution.py:215
  760.2 42.4 %copy-start.24 = (bf16[1536]{0:T(1024)(128)(2,1)S(1)}, bf16[1536]{0:T(1024)(128)(2,1)}, u32[]{:S(2)}) copy-start(bf16[1536]{0:T(1024)(128)(2,1)} %get-tuple-element.45) | copy-start | bytes 9220
  760.2 66.6 %copy-start.4 = (f32[128,1536]{1,0:T(8,128)S(1)}, f32[128,1536]{1,0:T(8,128)}, u32[]{:S(2)}) copy-start(f32[128,1536]{1,0:T(8,128)} %copy-done.3) | copy-start | bytes 2359300
  760.2 66.6 %copy-start.34 = (f32[128]{0:T(128)S(1)}, f32[128]{0:T(128)}, u32[]{:S(2)}) copy-start(f32[128]{0:T(128)} %get-tuple-element.79) | copy-start | bytes 1540
  760.2 208.4 %all-gather.18.cloned.1.call-start = ((), (), s32[]{:S(2)}) async-start(), calls=%async_computation.18 | async-start | bytes 12902400 | tf_op jit(solution)/shard_map/all_gather | solution.py:175
  863.3 3.4 copy-start.13
  989.4 6.9 copy-start
  (8 other events, 7.9 us)
Sparse Core Ops, SparseCore 0:
  10.2 66.9 all-gather.9
  78.7 48.5 all-gather.11
  130.9 17.7 all-reduce.8
  152.0 97.6 all-gather.13
  252.9 67.3 all-gather.15
  337.0 113.5 reduce-scatter.12
  456.7 113.9 reduce-scatter.10
  580.6 23.2 reduce-scatter.18
  606.2 71.1 reduce-scatter.16
  680.1 79.9 reduce-scatter.14
  763.0 18.2 reduce-scatter.20
  784.1 17.0 all-reduce.10
  804.3 58.8 all-reduce.12
  865.0 103.5 all-gather.17
where the time goes:
time: 1050 us
  waiting for transfers between devices  663 us (63%)
  blocking collectives  162 us (15%)
  local copies, waits for them, and re-layouts  105 us (10%)
  matrix products  63.1 us (6%)
  other arithmetic  32.7 us (3%)
  between operations  15.3 us (1%)
    reduce_scatter x2, waiting for transfers between devices, scatter_sum(): lax.psum_scatter(partial_sum.astype(bf16), everyone, scatter_dimension=0,...  222 us
    reduce_scatter x2, waiting for transfers between devices, total(): lax.psum_scatter(partial_sum.astype(bf16), 'shard', scatter_dimension=0,...  126 us
    all_gather x1, waiting for transfers between devices, body(): made = lax.all_gather(made, 'ctx', axis=0, tiled=False)  101 us
    all_to_all x1, blocking collectives, body(): lax.all_to_all(mine, 'shard', split_axis=0, concat_axis=0, tiled=True)  85.7 us
    unnamed x98, local copies, waits for them, and re-layouts  74.5 us
    all_gather x1, waiting for transfers between devices, body(): grad_all = lax.all_gather(my_half(grad_rows), everyone, axis=0, tiled=True)  42.8 us
    unnamed x16, waiting for transfers between devices  40.1 us
    all_gather x1, waiting for transfers between devices, body(): lax.all_gather(w_attn_out, 'shard', axis=0, tiled=True)  36.5 us
  transfers between devices with their start and end apart: 15, of which 13 were waited for; matrix products, arithmetic and copies ran while one was open for 9% of the time, Pallas kernels for 0%

commit v1 on v0

--- a/solution.py
+++ b/solution.py
@@ -6,6 +6,28 @@
 EPSILON = 1e-06
 ROPE_BASE = 1000000.0
 NEGATIVE = -1e30
+
+
+def in_order(blocks, dim):
+    shape = list(blocks.shape[1:])
+    shape[dim] *= blocks.shape[0]
+    return jnp.moveaxis(blocks, 0, dim).reshape(shape)
+
+
+def grow_blocks(value, axis):
+    size = lax.axis_size(axis)
+    parts = value[None]
+    for level in range(size.bit_length() - 1):
+        apart = 1 << level
+        partner_block = lax.ppermute(parts, axis, [(i, i ^ apart) for i in range(size)])
+        both = jnp.stack([parts, partner_block])
+        upper = lax.axis_index(axis) >> level & 1
+        parts = jnp.where(upper == 0, both, both[::-1]).reshape(-1, *value.shape)
+    return parts
+
+
+def gather_by_bits(x, axis, dim):
+    return in_order(grow_blocks(x, axis), dim)
 
 
 def rope_tables(positions, head_dim):
@@ -78,7 +100,7 @@
     bf16 = jnp.bfloat16
     qkv_full, attn_out_full, gain_one_bf, bias_full, gain_two_bf = (
         lax.all_gather(w_qkv, "shard", axis=0, tiled=True),
-        lax.all_gather(w_attn_out, "shard", axis=0, tiled=True),
+        gather_by_bits(w_attn_out, "shard", 0),
         lax.all_gather(norm1_gain, "shard", axis=0, tiled=True),
         lax.all_gather(b_qkv, "shard", axis=0, tiled=True),
         lax.all_gather(norm2_gain, "shard", axis=0, tiled=True),

time: 1050 us -> 1080 us (1.029)
  blocking collectives: 162 us -> 251 us
  waiting for transfers between devices: 663 us -> 593 us
    all_gather x1, blocking collectives: 15.2 us -> 80.1 us  [body(): lax.all_gather(b_qkv, 'shard', axis=0, tiled=True)]
    all_gather x1 -> x0, waiting for transfers between devices: 36.5 us -> none  [body(): lax.all_gather(w_attn_out, 'shard', axis=0, tiled=True)]
    all_gather x1, waiting for transfers between devices: 35.5 us -> 0.02 us  [body(): lax.all_gather(w_qkv, 'shard', axis=0, tiled=True)]
    all_gather x1, blocking collectives: 13.6 us -> 37.7 us  [body(): lax.all_gather(norm1_gain, 'shard', axis=0, tiled=True)]
    unnamed x16 -> x15, waiting for transfers between devices: 40.1 us -> 40.7 us
  transfers between devices with their start and end apart: 15 -> 16, of which waited for: 13 -> 11; matrix products, arithmetic and copies ran while one was open for 9% -> 9% of each run, Pallas kernels for 0% -> 0%
where the time goes in v1:
time: 1080 us; the launch traced here: 1070 us
  waiting for transfers between devices  593 us (55%)
  blocking collectives  251 us (23%)
  local copies, waits for them, and re-layouts  108 us (10%)
  matrix products  63.8 us (6%)
  other arithmetic  33.7 us (3%)
  between operations  15.3 us (1%)
    reduce_scatter x2, waiting for transfers between devices, scatter_sum(): lax.psum_scatter(partial_sum.astype(bf16), everyone, scatter_dimension=0,...  220 us
    reduce_scatter x2, waiting for transfers between devices, total(): lax.psum_scatter(partial_sum.astype(bf16), 'shard', scatter_dimension=0,...  130 us
    all_gather x1, waiting for transfers between devices, body(): made = lax.all_gather(made, 'ctx', axis=0, tiled=False)  101 us
    all_to_all x1, blocking collectives, body(): lax.all_to_all(mine, 'shard', split_axis=0, concat_axis=0, tiled=True)  85.4 us
    all_gather x1, blocking collectives, body(): lax.all_gather(b_qkv, 'shard', axis=0, tiled=True)  80.1 us
    unnamed x98, local copies, waits for them, and re-layouts  75.6 us
    all_gather x1, waiting for transfers between devices, body(): grad_all = lax.all_gather(my_half(grad_rows), everyone, axis=0, tiled=True)  42 us
    unnamed x15, waiting for transfers between devices  40.7 us
  transfers between devices with their start and end apart: 16, of which 11 were waited for; matrix products, arithmetic and copies ran while one was open for 9% of the time, Pallas kernels for 0%

profile of v1, /device:TPU:0, one launch (start us, length us, event | category | flops | bytes accessed | tf_op | source)
XLA Modules:
  0.0 1073.5 jit_solution(9779028314949828245)
XLA Ops:
  7.3 2.5 copy.67
  9.8 3.1 collective-permute-start
  12.9 37.7 %all-gather.2 = bf16[4,1,384]{2,1,0:T(2,128)(2,1)S(1)} all-gather(bf16[1,1,384]{2,1,0:T(2,128)(2,1)S(1)} %reshape.570), channel_id=1, replica_groups=mesh['shard'=4,'ctx'=4,'tp'=2] {'shard'}, dimensions={0}, use_global_device_ids=true | all-gather | bytes 3840 | tf_op jit(solution)/shard_map/all_gather | solution.py:104
  51.6 80.1 %all_gather.35 = bf16[128,1,8]{2,1,0:T(2,128)(2,1)S(1)} all-gather(bf16[32,1,8]{2,1,0:T(2,128)(2,1)S(1)} %copy.68), channel_id=1, replica_groups=mesh['shard'=4,'ctx'=4,'tp'=2] {'shard'}, dimensions={0}, use_global_device_ids=true | all-gather | bytes 2560 | tf_op jit(solution)/shard_map/all_gather | solution.py:105
  136.4 2.9 fusion.49
  139.7 9.0 all_gather.36
  148.8 2.8 fusion.91
  155.2 1.8 fusion.92
  157.1 11.9 %all-gather.3 = bf16[4,1,384]{2,1,0:T(2,128)(2,1)S(1)} all-gather(bf16[1,1,384]{2,1,0:T(2,128)(2,1)S(1)} %reshape.572), channel_id=1, replica_groups=mesh['shard'=4,'ctx'=4,'tp'=2] {'shard'}, dimensions={0}, use_global_device_ids=true | all-gather | bytes 3840 | tf_op jit(solution)/shard_map/all_gather | solution.py:106
  169.1 6.5 all-reduce.9.cloned.1.call-done
  180.6 5.9 copy.73
  186.5 18.0 %copy.72 = bf16[384,2,4480]{0,2,1:T(8,128)(2,1)} copy(bf16[384,2,4480]{2,1,0:T(2,128)(2,1)} %param.17) | data formatting | bytes 13762560 | tf_op args[7]
  207.9 85.4 %all_to_all.10 = bf16[4,384,3,280]{1,3,2,0:T(8,128)(2,1)S(1)} all-to-all(bf16[4,384,3,280]{1,3,2,0:T(8,128)(2,1)S(1)} %copy.74), channel_id=1, replica_groups=mesh['shard'=4,'ctx'=4,'tp'=2] {'shard'}, dimensions={0} | all-to-all | bytes 5160960 | tf_op jit(solution)/shard_map/all_to_all | solution.py:122
  296.4 9.2 fusion.93
  305.6 42.0 %all-gather.13.cloned.1.call-done = bf16[1,2048,1536]{2,1,0:T(8,128)(2,1)} async-done(((bf16[1,64,1536]{2,1,0:T(8,128)(2,1)}), bf16[1,2048,1536]{2,1,0:T(8,128)(2,1)}) %all-gather.13.cloned.1.call-update) | async-done | bytes 6291472 | tf_op jit(solution)/shard_map/all_gather | solution.py:127
  347.6 8.1 multiply_convert_fusion.1
  357.1 7.0 convolution_convert_fusion
  364.2 7.7 convolution_convert_fusion.1
  372.0 2.5 copy.76
  374.4 103.4 %reduce-scatter.13.cloned.1.call-done = bf16[64,1536]{1,0:T(8,128)(2,1)} async-done(((bf16[2048,1536]{1,0:T(8,128)(2,1)}), bf16[64,1536]{1,0:T(8,128)(2,1)}) %reduce-scatter.13.cloned.1.call-update) | async-done | bytes 196624 | tf_op jit(solution)/shard_map/reduce_scatter | solution.py:186
  477.8 2.3 all_gather.41
  481.6 116.3 %reduce-scatter.11.cloned.1.call-done = bf16[64,1536]{1,0:T(8,128)(2,1)} async-done(((bf16[2048,1536]{1,0:T(8,128)(2,1)}), bf16[64,1536]{1,0:T(8,128)(2,1)}) %reduce-scatter.11.cloned.1.call-update) | async-done | bytes 196624 | tf_op jit(solution)/shard_map/reduce_scatter | solution.py:186
  597.9 2.5 all_gather.39
  601.6 2.6 multiply_reduce_fusion.1
  606.7 2.2 convolution_convert_fusion.3
  609.9 20.2 %reduce-scatter.19.cloned.1.call-done = bf16[128,256]{1,0:T(8,128)(2,1)} async-done(((bf16[512,256]{1,0:T(8,128)(2,1)}), bf16[128,256]{1,0:T(8,128)(2,1)}) %reduce-scatter.19.cloned.1.call-update) | async-done | bytes 65552
  631.2 2.8 fusion.5
  634.0 5.2 fusion.8
  639.2 6.5 convolution_convert_fusion.4
  647.6 4.6 all-to-all-start.1
  653.3 3.4 fusion.11
  656.7 48.0 %reduce-scatter.17.cloned.1.call-done = bf16[384,768]{1,0:T(8,128)(2,1)} async-done(((bf16[1536,768]{1,0:T(8,128)(2,1)}), bf16[384,768]{1,0:T(8,128)(2,1)}) %reduce-scatter.17.cloned.1.call-update) | async-done | bytes 589840 | tf_op jit(solution)/shard_map/reduce_scatter | solution.py:236
  704.7 81.7 %reduce-scatter.15.cloned.1.call-done = bf16[384,1,8,128]{3,0,2,1:T(8,128)(2,1)} async-done(((bf16[1536,1,8,128]{3,0,2,1:T(8,128)(2,1)}), bf16[384,1,8,128]{3,0,2,1:T(8,128)(2,1)}) %reduce-scatter.15.cloned.1.call-update) | async-done | bytes 786448 | tf_op jit(solution)/shard_map/reduce_scatter | solution.py:236
  788.4 19.6 %reduce-scatter.21.cloned.1.call-done = bf16[32,8]{1,0:T(8,128)(2,1)} async-done(((bf16[128,8]{1,0:T(8,128)(2,1)}), bf16[32,8]{1,0:T(8,128)(2,1)}) %reduce-scatter.21.cloned.1.call-update) | async-done | bytes 528
  808.8 19.3 %all-reduce.11.cloned.1.call-done = f32[128,1536]{1,0:T(8,128)} async-done(((f32[128,1536]{1,0:T(8,128)}), f32[128,1536]{1,0:T(8,128)}) %all-reduce.11.cloned.1.call-update) | async-done | bytes 786448 | tf_op jit(solution)/shard_map/psum | solution.py:68
  829.4 12.2 %all-reduce.4 = (bf16[1536]{0:T(1024)(128)(2,1)S(1)}, bf16[1536]{0:T(1024)(128)(2,1)S(1)}) all-reduce(bf16[1536]{0:T(1024)(128)(2,1)S(1)} %get-tuple-element.47, bf16[1536]{0:T(1024)(128)(2,1)S(1)} %copy-done.23), channel_id=7, replica_groups=mesh['shard'=4,'ctx'=4,'tp'=2] {'shard'}, use_global_device_ids=true, to_apply=%region_13.14.clone | all-reduce | flops 3072 | bytes 12288
  841.8 10.1 all-reduce.2
  853.6 2.4 fusion.39
  856.0 34.0 %all-reduce.13.cloned.1.call-done = (bf16[384,1,8,128]{3,0,2,1:T(8,128)(2,1)}, bf16[384,768]{1,0:T(8,128)(2,1)}) async-done(((bf16[384,1,8,128]{3,0,2,1:T(8,128)(2,1)}, bf16[384,768]{1,0:T(8,128)(2,1)}), (bf16[384,1,8,128]{3,0,2,1:T(8,128)(2,1)}, bf16[384,768]{1,0:T(8,128)(2,1)})) %all-reduce.13.cloned.1.call-update) | async-done | bytes 1376272 | tf_op jit(solution)/shard_map/psum | solution.py:237
  891.4 2.1 copy.85
  894.5 100.9 %all-gather.15.cloned.1.call-done = bf16[16,384,840]{1,2,0:T(8,128)(2,1)} async-done(((bf16[4,384,840]{1,2,0:T(8,128)(2,1)}), bf16[16,384,840]{1,2,0:T(8,128)(2,1)}) %all-gather.15.cloned.1.call-update) | async-done | bytes 10321936 | tf_op jit(solution)/shard_map/all_gather | solution.py:197
  995.5 12.6 %convert_multiply_fusion = f32[16,384,840]{1,2,0:T(8,128)} fusion(bf16[16,384,840]{1,2,0:T(8,128)(2,1)} %all-gather.15.cloned.1.call-done), kind=kLoop, calls=%fused_computation.1 | loop fusion | flops 10321920 | bytes 30965760 | tf_op jit(solution)/shard_map/mul | solution.py:200
  1008.1 8.2 copy.84
  1016.3 6.9 copy-done
  1023.2 3.2 slice_bitcast_fusion
  1026.4 10.7 slice.106
  1037.1 21.5 %copy.86 = f32[384,2,4480]{2,1,0:T(2,128)} copy(f32[384,2,4480]{0,2,1:T(8,128)} %slice.106) | data formatting | bytes 27525120
  1058.6 8.4 copy.87
  (190 shorter events, 40.5 us)
Async XLA Ops:
  7.2 2.6 copy-start.19
  7.2 5.7 copy-start.31
  7.2 43.5 %copy-start.33 = (s32[1,128]{1,0:T(1,128)S(1)}, s32[1,128]{1,0:T(1,128)}, u32[]{:S(2)}) copy-start(s32[1,128]{1,0:T(1,128)} %param.11) | copy-start | bytes 1540
  7.2 129.2 %all-gather.9.cloned.1.call-start = ((), (), s32[]{:S(2)}) async-start(), calls=%async_computation.8 | async-start | bytes 3932160 | tf_op jit(solution)/shard_map/all_gather | solution.py:102
  9.7 165.9 %all-reduce.9.cloned.1.call-start = ((), (), s32[]{:S(2)}) async-start(), calls=%async_computation.9 | async-start | bytes 1572864 | tf_op jit(solution)/shard_map/psum | solution.py:68
  9.8 40.9 %collective-permute-start = (bf16[1,384,768]{2,1,0:T(8,128)(2,1)S(1)}, bf16[1,384,768]{2,1,0:T(8,128)(2,1)S(1)}, u32[]{:S(2)}, u32[]{:S(2)}) collective-permute-start(bf16[1,384,768]{2,1,0:T(8,128)(2,1)S(1)} %bitcast.268), channel_id=1, source_target_pairs={{0,8},{8,0},{16,24},{24,16},{1,9},{9,1},{17,25},{25,17},{2,10},{10... | collective-permute-start | bytes 1769480 | tf_op jit(solution)/shard_map/ppermute | solution.py:22
  50.9 81.8 %copy-start.1 = (bf16[1,128,1536]{2,1,0:T(8,128)(2,1)S(1)}, bf16[1,128,1536]{2,1,0:T(8,128)(2,1)}, u32[]{:S(2)}) copy-start(bf16[1,128,1536]{2,1,0:T(8,128)(2,1)} %param.10) | copy-start | bytes 1179652
  51.1 83.3 %collective-permute-start.1 = (bf16[2,384,768]{2,1,0:T(8,128)(2,1)S(1)}, bf16[2,384,768]{2,1,0:T(8,128)(2,1)}, u32[]{:S(2)}, u32[]{:S(2)}) collective-permute-start(bf16[2,384,768]{2,1,0:T(8,128)(2,1)S(1)} %get-tuple-element.66), channel_id=1, source_target_pairs={{0,16},{8,24},{16,0},{24,8},{1,17},{9,25},{17,1},{25,9},{2,18},{10... | collective-permute-start | bytes 3538952 | tf_op jit(solution)/shard_map/ppermute | solution.py:22
  132.7 16.0 %copy-start.15 = (f32[128,128]{0,1:T(8,128)}, f32[128,128]{0,1:T(8,128)S(1)}, u32[]{:S(2)}) copy-start(f32[128,128]{0,1:T(8,128)S(1)} %get-tuple-element.89) | copy-start | bytes 196612
  132.7 16.0 %copy-start.17 = (f32[128,128]{0,1:T(8,128)}, f32[128,128]{0,1:T(8,128)S(1)}, u32[]{:S(2)}) copy-start(f32[128,128]{0,1:T(8,128)S(1)} %get-tuple-element.90) | copy-start | bytes 196612
  133.5 3.0 copy-start.24
  133.6 6.0 copy-start.20
  148.7 4.5 copy-start.9
  148.8 4.4 copy-start.12
  151.6 5.4 copy-start.26
  154.6 2.6 copy-start.32
  157.1 139.4 %all-gather.11.cloned.1.call-start = ((), (), s32[]{:S(2)}) async-start(), calls=%async_computation.10 | async-start | bytes 6488064 | tf_op jit(solution)/shard_map/all_gather | solution.py:174
  178.8 168.8 %all-gather.13.cloned.1.call-start = ((), (), s32[]{:S(2)}) async-start(), calls=%async_computation.16 | async-start | bytes 6488064 | tf_op jit(solution)/shard_map/all_gather | solution.py:127
  180.5 297.3 %reduce-scatter.13.cloned.1.call-start = ((), (), s32[]{:S(2)}) async-start(), calls=%async_computation.12 | async-start | bytes 6488064 | tf_op jit(solution)/shard_map/reduce_scatter | solution.py:186
  293.6 1.5 copy-start.2
  347.6 9.4 copy-start.7
  364.1 233.7 %reduce-scatter.11.cloned.1.call-start = ((), (), s32[]{:S(2)}) async-start(), calls=%async_computation.11 | async-start | bytes 6488064 | tf_op jit(solution)/shard_map/reduce_scatter | solution.py:186
  371.9 258.2 %reduce-scatter.19.cloned.1.call-start = ((), (), s32[]{:S(2)}) async-start(), calls=%async_computation.18 | async-start | bytes 327680
  374.4 225.9 %copy-start.11 = (bf16[1,128,1536]{2,1,0:T(8,128)(2,1)S(1)}, bf16[1,128,1536]{2,1,0:T(8,128)(2,1)}, u32[]{:S(2)}) copy-start(bf16[1,128,1536]{2,1,0:T(8,128)(2,1)} %param.19) | copy-start | bytes 1179652
  374.4 225.9 %copy-start.29 = (f32[128]{0:T(128)S(1)}, f32[128]{0:T(128)}, u32[]{:S(2)}) copy-start(f32[128]{0:T(128)} %copy-done.28) | copy-start | bytes 1540
  374.4 225.9 %copy-start.34 = (f32[128]{0:T(128)S(1)}, f32[128]{0:T(128)}, u32[]{:S(2)}) copy-start(f32[128]{0:T(128)} %get-tuple-element.83) | copy-start | bytes 1540
  481.6 120.0 %copy-start.6 = (bf16[6,128,128]{1,2,0:T(8,128)(2,1)S(1)}, bf16[6,128,128]{1,2,0:T(8,128)(2,1)}, u32[]{:S(2)}) copy-start(bf16[6,128,128]{1,2,0:T(8,128)(2,1)} %copy-done.5) | copy-start | bytes 589828
  601.6 2.6 copy-start.4
  601.6 2.9 copy-start.8
  601.6 2.9 copy-start.10
  601.6 2.9 copy-start.27
  606.6 98.0 %reduce-scatter.17.cloned.1.call-start = ((), (), s32[]{:S(2)}) async-start(), calls=%async_computation.15 | async-start | bytes 2949120 | tf_op jit(solution)/shard_map/reduce_scatter | solution.py:236
  608.9 22.2 %copy-start.22 = (f32[128,1,64]{0,2,1:T(8,128)S(1)}, f32[128,1,64]{0,2,1:T(8,128)}, u32[]{:S(2)}) copy-start(f32[128,1,64]{0,2,1:T(8,128)} %get-tuple-element.77) | copy-start | bytes 98308
  608.9 22.2 %copy-start.21 = (f32[128,1,1,64]{0,3,2,1:T(8,128)S(1)}, f32[128,1,1,64]{0,3,2,1:T(8,128)}, u32[]{:S(2)}) copy-start(f32[128,1,1,64]{0,3,2,1:T(8,128)} %copy-done.20) | copy-start | bytes 98308
  608.9 177.5 %reduce-scatter.15.cloned.1.call-start = ((), (), s32[]{:S(2)}) async-start(), calls=%async_computation.14 | async-start | bytes 3932160 | tf_op jit(solution)/shard_map/reduce_scatter | solution.py:236
  609.7 21.5 %copy-start.25 = (f32[128]{0:T(128)S(1)}, f32[128]{0:T(128)}, u32[]{:S(2)}) copy-start(f32[128]{0:T(128)} %copy-done.24) | copy-start | bytes 1540
  634.0 5.2 copy-start.38
  634.0 5.2 copy-start.40
  647.6 138.9 %all-to-all-start.1 = ((bf16[4,384,840]{1,2,0:T(8,128)(2,1)}), bf16[4,384,840]{1,2,0:T(8,128)(2,1)}, u32[]{:S(2)}, u32[]{:S(2)}) async-start(bf16[4,384,840]{1,2,0:T(8,128)(2,1)} %bitcast.250), calls=%async_computation.5 | async-start | bytes 5160960 | tf_op jit(solution)/shard_map/all_to_all | solution.py:196
  652.2 155.8 %reduce-scatter.21.cloned.1.call-start = ((), (), s32[]{:S(2)}) async-start(), calls=%async_computation.19 | async-start | bytes 40960
  653.2 174.9 %all-reduce.11.cloned.1.call-start = ((), (), s32[]{:S(2)}) async-start(), calls=%async_computation.13 | async-start | bytes 1572864 | tf_op jit(solution)/shard_map/psum | solution.py:68
  656.6 130.5 %copy-start.36 = (u32[32]{0:T(128)S(1)}, u32[32]{0:T(128)}, u32[]{:S(2)}) copy-start(u32[32]{0:T(128)} %constant.67) | copy-start | bytes 388
  656.7 233.3 %all-reduce.13.cloned.1.call-start = ((), (), s32[]{:S(2)}) async-start(), calls=%async_computation.20 | async-start | bytes 2752512 | tf_op jit(solution)/shard_map/psum | solution.py:237
  786.4 43.0 %copy-start.23 = (bf16[1536]{0:T(1024)(128)(2,1)S(1)}, bf16[1536]{0:T(1024)(128)(2,1)}, u32[]{:S(2)}) copy-start(bf16[1536]{0:T(1024)(128)(2,1)} %get-tuple-element.45) | copy-start | bytes 9220
  786.4 67.2 %copy-start.35 = (f32[128]{0:T(128)S(1)}, f32[128]{0:T(128)}, u32[]{:S(2)}) copy-start(f32[128]{0:T(128)} %get-tuple-element.81) | copy-start | bytes 1540
  786.4 209.0 %all-gather.15.cloned.1.call-start = ((), (), s32[]{:S(2)}) async-start(), calls=%async_computation.17 | async-start | bytes 12902400 | tf_op jit(solution)/shard_map/all_gather | solution.py:197
  890.0 3.4 copy-start.14
  1016.3 6.9 copy-start
  (9 other events, 7.9 us)
Sparse Core Ops, SparseCore 0:
  10.2 104.1 all-gather.8
  157.2 18.3 all-reduce.8
  179.1 96.6 all-gather.10
  279.1 68.5 all-gather.12
  364.3 113.4 reduce-scatter.12
  483.9 113.9 reduce-scatter.10
  606.8 23.3 reduce-scatter.18
  632.4 72.2 reduce-scatter.16
  707.6 78.7 reduce-scatter.14
  789.1 18.9 reduce-scatter.20
  810.9 17.1 all-reduce.10
  831.1 58.9 all-reduce.12
  891.9 103.5 all-gather.14
